TPU v7x, 32 devices: a whole 2x2x4 slice. The times are simulated.
32 devices in a mesh: grp: 2 (over x), seq: 16 (over z, y, core).
Axes of the slice: x: 2, y: 2, z: 4, core: 2. Of those that a mesh axis runs over, the one named last changes fastest.
Arguments:
- llm_grad: bfloat16 [4096, 8192], P('seq', 'grp'), may hold values from -6 to 6
- image_grid: int32 [256, 2], replicated, may hold values from 1 to 3, as said below
- image_owner: int32 [256], replicated, may hold values from 0 to 15, as said below
- row_start: int32 [256], replicated, may hold values from 0 to 255, as said below
- merger_pre: bfloat16 [48, 16, 2560], P(None, 'seq', 'grp'), may hold values from -6 to 6
- vit_out: bfloat16 [192, 16, 1280], P(None, 'seq'), may hold values from -6 to 6
- vit_pre: bfloat16 [192, 16, 2560], P(None, 'seq', 'grp'), may hold values from -6 to 6
- ln_gain: float32 [1280], replicated, may hold values from 0.25 to 1.75
- merger_out_w: bfloat16 [8192, 2560], P('seq', 'grp'), may hold values from -0.0625 to 0.0625
- merger_in_w: bfloat16 [2560, 5120], P('grp', 'seq'), may hold values from -0.125 to 0.125
- vit_fc2_w: bfloat16 [1280, 2560], P('seq', 'grp'), may hold values from -0.15625 to 0.15625
Outputs:
- patch_grad: bfloat16 [192, 16, 1280], P('grp', 'seq')
- fc1_grad: bfloat16 [192, 16, 2560], P(None, 'seq', 'grp')
- fc2_w_grad: float32 [1280, 2560], P('seq', 'grp')
Inputs may be any that keep to these rules, and one draw needn't show every extreme that they name: `image_grid`: height times width is 1 to 3; the first image of every shard is 1 by 3; the last image of shard 0 is 1 by 1. `image_owner`: the 16 images of one shard have 16 different owners. An image's rows row_start to row_start + t - 1 lie inside its shard and meet no other image's rows; a shard's images follow the order of k; the last image of every shard ends at the shard's last row; the first image of shard 0 starts at row 0.
All inputs are finite; a program needn't handle non-finite values.
Results may differ from a plain program's by a relative error of at most 0.02.
Values may be sent and summed in bfloat16 or wider, within the bound.
A program may use at most 128 MiB of HBM per device.

v0:
```python
import jax
import jax.numpy as jnp
from jax import lax
from jax.sharding import PartitionSpec as P

SLOT = 3


def gelu_slope(values):
    return (
        0.5 * (1.0 + lax.erf(values * 0.7071067811865476))
        + values * jnp.exp(-0.5 * values * values) * 0.3989422804014327
    )


def patch_table(widths, counts, slots):
    places = jnp.arange(4 * slots, dtype=jnp.int32)
    merged = places // 4
    corner = places % 4
    row_in = merged[None, :] // widths[:, None]
    col_in = merged[None, :] % widths[:, None]
    target = (
        (2 * row_in + corner[None, :] // 2) * (2 * widths[:, None])
        + 2 * col_in
        + corner[None, :] % 2
    )
    usable = merged[None, :] < counts[:, None]
    return ((target[:, None, :] == places[None, :, None]) & usable[:, None, :]).astype(jnp.float32)


def norm_backward(upstream, inputs, scales):
    average = jnp.mean(inputs, -1, keepdims=True)
    centred = inputs - average
    inverse_std = lax.rsqrt(jnp.mean(centred * centred, -1, keepdims=True) + 1e-06)
    normed = centred * inverse_std
    scaled = upstream * scales
    return inverse_std * (
        scaled
        - jnp.mean(scaled, -1, keepdims=True)
        - normed * jnp.mean(scaled * normed, -1, keepdims=True)
    )


def on_device(
    llm_grad,
    image_grid,
    image_owner,
    row_start,
    merger_pre,
    vit_out,
    vit_pre,
    ln_gain,
    merger_out_w,
    merger_in_w,
    vit_fc2_w,
):
    seq_count = lax.axis_size("seq")
    own_index = lax.axis_index("seq")
    grids = image_grid.reshape(seq_count, seq_count, 2)
    counts = grids[:, :, 0] * grids[:, :, 1]
    widths = grids[:, :, 1]
    owners = image_owner.reshape(seq_count, seq_count)
    starts = row_start.reshape(seq_count, seq_count)
    within = jnp.arange(SLOT, dtype=jnp.int32)
    peers = jnp.arange(seq_count, dtype=jnp.int32)
    shard_rows = llm_grad.shape[0]
    my_owners = lax.dynamic_index_in_dim(owners, own_index, 0, keepdims=False)
    my_counts = lax.dynamic_index_in_dim(counts, own_index, 0, keepdims=False)
    my_starts = lax.dynamic_index_in_dim(starts, own_index, 0, keepdims=False)
    targets = (my_owners[None, :] == peers[:, None]).astype(jnp.int32)
    send_counts = jnp.sum(targets * my_counts[None, :], 1)
    send_starts = jnp.sum(targets * my_starts[None, :], 1)
    indices = jnp.minimum(send_starts[:, None] + within[None, :], shard_rows - 1)
    usable = within[None, :] < send_counts[:, None]
    picked = jnp.take(llm_grad, indices.reshape(-1), axis=0)
    outgoing = jnp.where(usable.reshape(-1, 1), picked, jnp.zeros_like(picked)).reshape(
        seq_count, SLOT, llm_grad.shape[1]
    )
    received = (owners == own_index).astype(jnp.int32)
    recv_counts = jnp.sum(received * counts, 1)
    recv_widths = jnp.sum(received * widths, 1)
    wide_rows = lax.all_gather(outgoing.reshape(-1, llm_grad.shape[1]), "grp", axis=1, tiled=True)
    sliced = lax.all_to_all(wide_rows, "seq", split_axis=1, concat_axis=0, tiled=True)
    features = sliced.shape[1]
    by_owner = jnp.swapaxes(sliced.reshape(seq_count, seq_count, SLOT, features), 0, 1).reshape(
        -1, features
    )
    folded = jnp.dot(by_owner, merger_out_w, preferred_element_type=jnp.float32)
    arrived = lax.all_to_all(
        folded.astype(jnp.bfloat16), "seq", split_axis=0, concat_axis=0, tiled=True
    )
    unit_grad = jnp.sum(
        arrived.reshape(seq_count, seq_count * SLOT, -1).astype(jnp.float32), 0
    ).astype(jnp.bfloat16)
    pre_act = merger_pre[:, 0, :].astype(jnp.float32)
    pre_grad = (gelu_slope(pre_act) * unit_grad.astype(jnp.float32)).astype(jnp.bfloat16)
    all_pre = lax.all_gather(pre_grad, "seq", axis=0, tiled=True)
    part_cols = jnp.dot(all_pre, merger_in_w, preferred_element_type=jnp.float32)
    part_rows = lax.all_to_all(
        part_cols.astype(jnp.bfloat16), "seq", split_axis=0, concat_axis=1, tiled=True
    )
    merged_part = jnp.sum(lax.all_gather(part_rows, "grp", axis=0).astype(jnp.float32), 0)
    vit_width = vit_out.shape[2]
    table = patch_table(recv_widths, recv_counts, SLOT)
    patch_in = jnp.einsum(
        "spq,sqc->spc",
        table,
        merged_part.reshape(seq_count, 4 * SLOT, vit_width),
        precision=lax.Precision.HIGHEST,
    ).reshape(-1, vit_width)
    patch_grad = norm_backward(patch_in, vit_out[:, 0, :].astype(jnp.float32), ln_gain).astype(
        jnp.bfloat16
    )
    group_rows = patch_grad.shape[0] // lax.axis_size("grp")
    own_rows = lax.dynamic_slice_in_dim(
        patch_grad, lax.axis_index("grp") * group_rows, group_rows, 0
    )
    columns = patch_grad
    act_grad = jnp.dot(
        columns,
        lax.all_gather(vit_fc2_w, "seq", axis=0, tiled=True),
        preferred_element_type=jnp.float32,
    )
    fc_in = vit_pre[:, 0, :].astype(jnp.float32)
    sigmoid_q = jax.nn.sigmoid(1.702 * fc_in)
    activation = (fc_in * sigmoid_q).astype(jnp.bfloat16)
    fc1_grad = ((sigmoid_q + 1.702 * fc_in * sigmoid_q * (1.0 - sigmoid_q)) * act_grad).astype(
        jnp.bfloat16
    )
    columns = patch_grad
    weight_part = lax.dot_general(
        columns, activation, (((0,), (0,)), ((), ())), preferred_element_type=jnp.float32
    )
    weight_parts = lax.all_to_all(
        weight_part.astype(jnp.bfloat16), "seq", split_axis=0, concat_axis=0, tiled=True
    )
    weight_grad = jnp.sum(
        weight_parts.reshape(seq_count, -1, weight_part.shape[1]).astype(jnp.float32), 0
    )
    return (
        own_rows.reshape(group_rows, 1, vit_width),
        fc1_grad.reshape(-1, 1, vit_pre.shape[2]),
        weight_grad,
    )


def solution(mesh):
    return jax.shard_map(
        on_device,
        mesh=mesh,
        in_specs=(
            P("seq", "grp"),
            P(),
            P(),
            P(),
            P(None, "seq", "grp"),
            P(None, "seq", None),
            P(None, "seq", "grp"),
            P(),
            P("seq", "grp"),
            P("grp", "seq"),
            P("seq", "grp"),
        ),
        out_specs=(P("grp", "seq", None), P(None, "seq", "grp"), P("seq", "grp")),
        check_vma=False,
    )
```

profile of v0, /device:TPU:13, one launch (start us, length us, event | category | flops | bytes accessed | tf_op | source)
XLA Modules:
  0.0 296.6 jit_solution(5290898509459888009)
XLA Ops:
  11.3 10.7 %all_gather.15 = bf16[48,8192]{1,0:T(8,128)(2,1)S(1)} all-gather(bf16[48,4096]{1,0:T(8,128)(2,1)S(1)} %select_select_fusion), channel_id=1, replica_groups=mesh['grp'=2,'seq'=16] {'grp'}, dimensions={1}, use_global_device_ids=true | all-gather | bytes 1179648 | tf_op jit(solution)/shard_map/all_gather | solution.py:82
  22.1 26.4 %all_to_all.50 = bf16[48,16,512]{2,0,1:T(8,128)(2,1)S(1)} all-to-all(bf16[48,16,512]{2,0,1:T(8,128)(2,1)S(1)} %bitcast.84), channel_id=1, replica_groups=mesh['grp'=2,'seq'=16] {'seq'}, dimensions={1} | all-to-all | bytes 1572864 | tf_op jit(solution)/shard_map/all_to_all | solution.py:83
  49.6 1.4 reshape.497
  51.0 2.7 convolution_convert_fusion.1
  53.7 49.2 %all_to_all.51 = bf16[16,48,1280]{2,1,0:T(8,128)(2,1)} all-to-all(bf16[16,48,1280]{2,1,0:T(8,128)(2,1)S(1)} %bitcast.85), channel_id=1, replica_groups=mesh['grp'=2,'seq'=16] {'seq'}, dimensions={0} | all-to-all | bytes 3932160 | tf_op jit(solution)/shard_map/all_to_all | solution.py:89
  103.0 1.9 reduce_sum.108
  106.9 38.0 %all-gather.3.cloned.1.call-done = bf16[768,1280]{1,0:T(8,128)(2,1)} async-done(((bf16[48,1280]{1,0:T(8,128)(2,1)}), bf16[768,1280]{1,0:T(8,128)(2,1)}) %all-gather.3.cloned.1.call-update) | async-done | bytes 1966096 | tf_op jit(solution)/shard_map/all_gather | solution.py:97
  144.9 2.6 convolution_convert_fusion.2
  148.5 6.4 %all-to-all-start.2 = ((bf16[16,48,320]{2,1,0:T(8,128)(2,1)}), bf16[16,48,320]{2,1,0:T(8,128)(2,1)}, u32[]{:S(2)}, u32[]{:S(2)}) async-start(bf16[16,48,320]{2,1,0:T(8,128)(2,1)} %bitcast.13), calls=%async_computation.2 | async-start | bytes 1179648 | tf_op jit(solution)/shard_map/all_to_all | solution.py:99
  155.0 1.1 reshape.503
  156.6 20.1 %all-to-all-done.2 = bf16[16,48,320]{2,1,0:T(8,128)(2,1)} async-done(((bf16[16,48,320]{2,1,0:T(8,128)(2,1)}), bf16[16,48,320]{2,1,0:T(8,128)(2,1)}, u32[]{:S(2)}, u32[]{:S(2)}) %all-to-all-start.2) | async-done | bytes 491552 | tf_op jit(solution)/shard_map/all_to_all | solution.py:99
  176.7 2.0 copy.23
  178.7 2.3 all_gather.17
  181.0 13.6 %all_gather.18 = bf16[2,48,5120]{2,1,0:T(8,128)(2,1)S(1)} all-gather(bf16[1,48,5120]{2,1,0:T(8,128)(2,1)} %all_gather.17), channel_id=1, replica_groups=mesh['grp'=2,'seq'=16] {'grp'}, dimensions={0}, use_global_device_ids=true | all-gather | bytes 1474560 | tf_op jit(solution)/shard_map/all_gather | solution.py:102
  195.8 2.5 reshape.498
  198.3 2.4 multiply_reduce_fusion.1
  201.8 1.3 multiply_convert_fusion
  203.1 1.2 convert_element_type.82
  204.3 3.9 %convolution_convert_fusion = bf16[1280,1280]{1,0:T(8,128)(2,1)} fusion(bf16[192,1280]{1,0:T(8,128)(2,1)S(1)} %convert_element_type.82, bf16[192,1,1280]{2,0,1:T(8,128)(2,1)} %param.17), kind=kOutput, calls=%fused_computation.1 | convolution fusion | flops 632504320 | bytes 4259840 | tf_op jit(solution)/shard_map/dot_general | solution.py:131
  208.1 5.6 %all-to-all-start.3 = ((bf16[16,80,1280]{2,1,0:T(8,128)(2,1)}), bf16[16,80,1280]{2,1,0:T(8,128)(2,1)}, u32[]{:S(2)}, u32[]{:S(2)}) async-start(bf16[16,80,1280]{2,1,0:T(8,128)(2,1)} %bitcast.81), calls=%async_computation.3 | async-start | bytes 6553600 | tf_op jit(solution)/shard_map/all_to_all | solution.py:134
  215.0 1.7 multiply_convert_fusion.1
  217.5 3.6 %fusion.1 = bf16[192,1,1280]{2,0,1:T(8,128)(2,1)} fusion(bf16[192,1280]{1,0:T(8,128)(2,1)S(1)} %multiply_convert_fusion.1, bf16[1280,1280]{1,0:T(8,128)(2,1)} %all-gather.5.cloned.1.call-done, bf16[192,1,1280]{2,0,1:T(8,128)(2,1)S(1)} %copy-done.6), kind=kOutput, calls=%fused_computation.6 | convolution fusion | flops 631848960 | bytes 4751360 | tf_op jit(solution)/shard_map/dot_general | solution.py:119
  221.1 65.5 %all-to-all-done.3 = bf16[16,80,1280]{2,1,0:T(8,128)(2,1)} async-done(((bf16[16,80,1280]{2,1,0:T(8,128)(2,1)}), bf16[16,80,1280]{2,1,0:T(8,128)(2,1)}, u32[]{:S(2)}, u32[]{:S(2)}) %all-to-all-start.3) | async-done | bytes 3276832 | tf_op jit(solution)/shard_map/all_to_all | solution.py:134
  286.6 3.2 %convert_reduce_fusion = f32[80,1280]{1,0:T(8,128)} fusion(bf16[16,80,1280]{2,1,0:T(8,128)(2,1)} %all-to-all-done.3), kind=kLoop, calls=%fused_computation.2 | loop fusion | flops 3174400 | bytes 3686400 | tf_op jit(solution)/shard_map/reduce_sum | solution.py:137
  (60 shorter events, 12.9 us)
Async XLA Ops:
  7.2 3.2 %copy-start = (bf16[256,4096]{1,0:T(8,128)(2,1)S(1)}, bf16[256,4096]{1,0:T(8,128)(2,1)}, u32[]{:S(2)}) copy-start(bf16[256,4096]{1,0:T(8,128)(2,1)} %param.11) | copy-start | bytes 6291460
  7.2 137.7 %all-gather.3.cloned.1.call-start = ((), (), s32[]{:S(2)}) async-start(), calls=%async_computation.4 | async-start | bytes 2088960 | tf_op jit(solution)/shard_map/all_gather | solution.py:97
  103.0 1.9 copy-start.4
  103.0 3.5 %copy-start.3 = (bf16[192,1,1280]{2,0,1:T(8,128)(2,1)S(1)}, bf16[192,1,1280]{2,0,1:T(8,128)(2,1)}, u32[]{:S(2)}) copy-start(bf16[192,1,1280]{2,0,1:T(8,128)(2,1)} %param.16) | copy-start | bytes 1474564
  105.7 111.8 %all-gather.5.cloned.1.call-start = ((), (), s32[]{:S(2)}) async-start(), calls=%async_computation.5 | async-start | bytes 3481600 | tf_op jit(solution)/shard_map/all_gather | solution.py:121
  148.5 28.2 %all-to-all-start.2 = ((bf16[16,48,320]{2,1,0:T(8,128)(2,1)}), bf16[16,48,320]{2,1,0:T(8,128)(2,1)}, u32[]{:S(2)}, u32[]{:S(2)}) async-start(bf16[16,48,320]{2,1,0:T(8,128)(2,1)} %bitcast.13), calls=%async_computation.2 | async-start | bytes 1179648 | tf_op jit(solution)/shard_map/all_to_all | solution.py:99
  195.8 2.6 copy-start.5
  200.7 1.1 copy-start.1
  208.1 5.7 %copy-start.2 = (f32[16,12,1280]{2,1,0:T(8,128)S(1)}, f32[16,12,1280]{2,1,0:T(8,128)}, u32[]{:S(2)}) copy-start(f32[16,12,1280]{2,1,0:T(8,128)} %copy-done.1) | copy-start | bytes 2949124
  208.1 78.4 %all-to-all-start.3 = ((bf16[16,80,1280]{2,1,0:T(8,128)(2,1)}), bf16[16,80,1280]{2,1,0:T(8,128)(2,1)}, u32[]{:S(2)}, u32[]{:S(2)}) async-start(bf16[16,80,1280]{2,1,0:T(8,128)(2,1)} %bitcast.81), calls=%async_computation.3 | async-start | bytes 6553600 | tf_op jit(solution)/shard_map/all_to_all | solution.py:134
  215.0 2.5 copy-start.6
Sparse Core Ops, SparseCore 0:
  105.8 39.0 all-gather.2
  147.2 52.0 all-gather.4
where the time goes:
time: 298 us; the launch traced here: 297 us
  waiting for transfers between devices  124 us (42%)
  blocking collectives  99.9 us (34%)
  local copies, waits for them, and re-layouts  19.6 us (7%)
  matrix products  15.2 us (5%)
  between operations  14.3 us (5%)
  starting transfers between devices  12.2 us (4%)
  other arithmetic  11.3 us (4%)
    all_to_all x1, waiting for transfers between devices, on_device(): lax.all_to_all(weight_part.astype(jnp.bfloat16), 'seq', split_axis=0, con...  65.5 us
    all_to_all x1, blocking collectives, on_device(): lax.all_to_all(folded.astype(jnp.bfloat16), 'seq', split_axis=0, concat_a...  49.2 us
    all_gather x1, waiting for transfers between devices, on_device(): all_pre = lax.all_gather(pre_grad, 'seq', axis=0, tiled=True)  38 us
    all_to_all x1, blocking collectives, on_device(): lax.all_to_all(wide_rows, 'seq', split_axis=1, concat_axis=0, tiled=True)  26.4 us
    all_to_all x1, waiting for transfers between devices, on_device(): lax.all_to_all(part_cols.astype(jnp.bfloat16), 'seq', split_axis=0, conca...  20.1 us
    all_gather x1, blocking collectives, on_device(): lax.all_gather(part_rows, 'grp', axis=0).astype(jnp.float32)  13.6 us
    all_gather x1, blocking collectives, on_device(): lax.all_gather(outgoing.reshape(-1, llm_grad.shape[1]), 'grp', axis=1, ti...  10.7 us
    all_to_all x1, starting transfers between devices, on_device(): lax.all_to_all(part_cols.astype(jnp.bfloat16), 'seq', split_axis=0, conca...  6.43 us
  transfers between devices with their start and end apart: 4, of which 3 were waited for; matrix products, arithmetic and copies ran while one was open for 9% of the time, Pallas kernels for 0%

commit v1 on v0

--- a/solution.py
+++ b/solution.py
@@ -80,7 +80,10 @@
     recv_counts = jnp.sum(received * counts, 1)
     recv_widths = jnp.sum(received * widths, 1)
     wide_rows = lax.all_gather(outgoing.reshape(-1, llm_grad.shape[1]), "grp", axis=1, tiled=True)
-    sliced = lax.all_to_all(wide_rows, "seq", split_axis=1, concat_axis=0, tiled=True)
+    sliced = jnp.concatenate(
+        lax.all_to_all(jnp.stack(jnp.split(wide_rows, lax.axis_size("seq"), axis=1)), "seq", 0, 0),
+        axis=0,
+    )
     features = sliced.shape[1]
     by_owner = jnp.swapaxes(sliced.reshape(seq_count, seq_count, SLOT, features), 0, 1).reshape(
         -1, features

time: 298 us -> 298 us (level)
  no operation moved by 1% of the time
where the time goes in v1:
time: 298 us; the launch traced here: 297 us
  waiting for transfers between devices  124 us (42%)
  blocking collectives  99.9 us (34%)
  local copies, waits for them, and re-layouts  19.6 us (7%)
  matrix products  15.2 us (5%)
  between operations  14.4 us (5%)
  starting transfers between devices  12.2 us (4%)
  other arithmetic  11.3 us (4%)
    all_to_all x1, waiting for transfers between devices, on_device(): lax.all_to_all(weight_part.astype(jnp.bfloat16), 'seq', split_axis=0, con...  65.5 us
    all_to_all x1, blocking collectives, on_device(): lax.all_to_all(folded.astype(jnp.bfloat16), 'seq', split_axis=0, concat_a...  49.2 us
    all_gather x1, waiting for transfers between devices, on_device(): all_pre = lax.all_gather(pre_grad, 'seq', axis=0, tiled=True)  38 us
    all_to_all x1, blocking collectives, on_device(): lax.all_to_all(jnp.stack(jnp.split(wide_rows, lax.axis_size('seq'), axis=...  26.4 us
    all_to_all x1, waiting for transfers between devices, on_device(): lax.all_to_all(part_cols.astype(jnp.bfloat16), 'seq', split_axis=0, conca...  20.1 us
    all_gather x1, blocking collectives, on_device(): lax.all_gather(part_rows, 'grp', axis=0).astype(jnp.float32)  13.6 us
    all_gather x1, blocking collectives, on_device(): lax.all_gather(outgoing.reshape(-1, llm_grad.shape[1]), 'grp', axis=1, ti...  10.7 us
    all_to_all x1, starting transfers between devices, on_device(): lax.all_to_all(part_cols.astype(jnp.bfloat16), 'seq', split_axis=0, conca...  6.44 us
  transfers between devices with their start and end apart: 4, of which 3 were waited for; matrix products, arithmetic and copies ran while one was open for 9% of the time, Pallas kernels for 0%

profile of v1, /device:TPU:13, one launch (start us, length us, event | category | flops | bytes accessed | tf_op | source)
XLA Modules:
  0.0 296.8 jit_solution(16084033416917905342)
XLA Ops:
  11.3 10.7 %all_gather.15 = bf16[48,8192]{1,0:T(8,128)(2,1)S(1)} all-gather(bf16[48,4096]{1,0:T(8,128)(2,1)S(1)} %select_select_fusion), channel_id=1, replica_groups=mesh['grp'=2,'seq'=16] {'grp'}, dimensions={1}, use_global_device_ids=true | all-gather | bytes 1179648 | tf_op jit(solution)/shard_map/all_gather | solution.py:82
  22.2 26.4 %all_to_all.39 = bf16[16,48,512]{2,1,0:T(8,128)(2,1)S(1)} all-to-all(bf16[16,48,512]{2,1,0:T(8,128)(2,1)S(1)} %fusion.32), channel_id=1, replica_groups=mesh['grp'=2,'seq'=16] {'seq'}, dimensions={0} | all-to-all | bytes 1572864 | tf_op jit(solution)/shard_map/all_to_all | solution.py:84
  49.7 1.4 reshape.489
  51.1 2.7 convolution_convert_fusion.1
  53.9 49.2 %all_to_all.40 = bf16[16,48,1280]{2,1,0:T(8,128)(2,1)} all-to-all(bf16[16,48,1280]{2,1,0:T(8,128)(2,1)S(1)} %bitcast.141), channel_id=1, replica_groups=mesh['grp'=2,'seq'=16] {'seq'}, dimensions={0} | all-to-all | bytes 3932160 | tf_op jit(solution)/shard_map/all_to_all | solution.py:92
  103.1 1.9 reduce_sum.108
  107.0 38.0 %all-gather.3.cloned.1.call-done = bf16[768,1280]{1,0:T(8,128)(2,1)} async-done(((bf16[48,1280]{1,0:T(8,128)(2,1)}), bf16[768,1280]{1,0:T(8,128)(2,1)}) %all-gather.3.cloned.1.call-update) | async-done | bytes 1966096 | tf_op jit(solution)/shard_map/all_gather | solution.py:100
  145.0 2.6 convolution_convert_fusion.2
  148.6 6.4 %all-to-all-start.2 = ((bf16[16,48,320]{2,1,0:T(8,128)(2,1)}), bf16[16,48,320]{2,1,0:T(8,128)(2,1)}, u32[]{:S(2)}, u32[]{:S(2)}) async-start(bf16[16,48,320]{2,1,0:T(8,128)(2,1)} %bitcast.28), calls=%async_computation.2 | async-start | bytes 1179648 | tf_op jit(solution)/shard_map/all_to_all | solution.py:102
  155.2 1.1 reshape.495
  156.7 20.1 %all-to-all-done.2 = bf16[16,48,320]{2,1,0:T(8,128)(2,1)} async-done(((bf16[16,48,320]{2,1,0:T(8,128)(2,1)}), bf16[16,48,320]{2,1,0:T(8,128)(2,1)}, u32[]{:S(2)}, u32[]{:S(2)}) %all-to-all-start.2) | async-done | bytes 491552 | tf_op jit(solution)/shard_map/all_to_all | solution.py:102
  176.8 2.0 copy.21
  178.8 2.3 all_gather.17
  181.1 13.6 %all_gather.18 = bf16[2,48,5120]{2,1,0:T(8,128)(2,1)S(1)} all-gather(bf16[1,48,5120]{2,1,0:T(8,128)(2,1)} %all_gather.17), channel_id=1, replica_groups=mesh['grp'=2,'seq'=16] {'grp'}, dimensions={0}, use_global_device_ids=true | all-gather | bytes 1474560 | tf_op jit(solution)/shard_map/all_gather | solution.py:105
  195.9 2.5 reshape.490
  198.4 2.4 multiply_reduce_fusion.1
  202.0 1.3 multiply_convert_fusion
  203.2 1.2 convert_element_type.82
  204.4 3.9 %convolution_convert_fusion = bf16[1280,1280]{1,0:T(8,128)(2,1)} fusion(bf16[192,1280]{1,0:T(8,128)(2,1)S(1)} %convert_element_type.82, bf16[192,1,1280]{2,0,1:T(8,128)(2,1)} %param.17), kind=kOutput, calls=%fused_computation.1 | convolution fusion | flops 632504320 | bytes 4259840 | tf_op jit(solution)/shard_map/dot_general | solution.py:134
  208.3 5.6 %all-to-all-start.3 = ((bf16[16,80,1280]{2,1,0:T(8,128)(2,1)}), bf16[16,80,1280]{2,1,0:T(8,128)(2,1)}, u32[]{:S(2)}, u32[]{:S(2)}) async-start(bf16[16,80,1280]{2,1,0:T(8,128)(2,1)} %bitcast.139), calls=%async_computation.3 | async-start | bytes 6553600 | tf_op jit(solution)/shard_map/all_to_all | solution.py:137
  215.2 1.7 multiply_convert_fusion.1
  217.6 3.6 %fusion.1 = bf16[192,1,1280]{2,0,1:T(8,128)(2,1)} fusion(bf16[192,1280]{1,0:T(8,128)(2,1)S(1)} %multiply_convert_fusion.1, bf16[1280,1280]{1,0:T(8,128)(2,1)} %all-gather.5.cloned.1.call-done, bf16[192,1,1280]{2,0,1:T(8,128)(2,1)S(1)} %copy-done.6), kind=kOutput, calls=%fused_computation.6 | convolution fusion | flops 631848960 | bytes 4751360 | tf_op jit(solution)/shard_map/dot_general | solution.py:122
  221.2 65.5 %all-to-all-done.3 = bf16[16,80,1280]{2,1,0:T(8,128)(2,1)} async-done(((bf16[16,80,1280]{2,1,0:T(8,128)(2,1)}), bf16[16,80,1280]{2,1,0:T(8,128)(2,1)}, u32[]{:S(2)}, u32[]{:S(2)}) %all-to-all-start.3) | async-done | bytes 3276832 | tf_op jit(solution)/shard_map/all_to_all | solution.py:137
  286.7 3.2 %convert_reduce_fusion = f32[80,1280]{1,0:T(8,128)} fusion(bf16[16,80,1280]{2,1,0:T(8,128)(2,1)} %all-to-all-done.3), kind=kLoop, calls=%fused_computation.2 | loop fusion | flops 3174400 | bytes 3686400 | tf_op jit(solution)/shard_map/reduce_sum | solution.py:140
  (75 shorter events, 13.0 us)
Async XLA Ops:
  7.2 3.2 %copy-start = (bf16[256,4096]{1,0:T(8,128)(2,1)S(1)}, bf16[256,4096]{1,0:T(8,128)(2,1)}, u32[]{:S(2)}) copy-start(bf16[256,4096]{1,0:T(8,128)(2,1)} %param.11) | copy-start | bytes 6291460
  7.2 137.8 %all-gather.3.cloned.1.call-start = ((), (), s32[]{:S(2)}) async-start(), calls=%async_computation.4 | async-start | bytes 2088960 | tf_op jit(solution)/shard_map/all_gather | solution.py:100
  103.1 1.9 copy-start.4
  103.1 3.5 %copy-start.3 = (bf16[192,1,1280]{2,0,1:T(8,128)(2,1)S(1)}, bf16[192,1,1280]{2,0,1:T(8,128)(2,1)}, u32[]{:S(2)}) copy-start(bf16[192,1,1280]{2,0,1:T(8,128)(2,1)} %param.16) | copy-start | bytes 1474564
  105.8 111.8 %all-gather.5.cloned.1.call-start = ((), (), s32[]{:S(2)}) async-start(), calls=%async_computation.5 | async-start | bytes 3481600 | tf_op jit(solution)/shard_map/all_gather | solution.py:124
  148.6 28.2 %all-to-all-start.2 = ((bf16[16,48,320]{2,1,0:T(8,128)(2,1)}), bf16[16,48,320]{2,1,0:T(8,128)(2,1)}, u32[]{:S(2)}, u32[]{:S(2)}) async-start(bf16[16,48,320]{2,1,0:T(8,128)(2,1)} %bitcast.28), calls=%async_computation.2 | async-start | bytes 1179648 | tf_op jit(solution)/shard_map/all_to_all | solution.py:102
  195.9 2.6 copy-start.5
  200.9 1.1 copy-start.1
  208.3 5.7 %copy-start.2 = (f32[16,12,1280]{2,1,0:T(8,128)S(1)}, f32[16,12,1280]{2,1,0:T(8,128)}, u32[]{:S(2)}) copy-start(f32[16,12,1280]{2,1,0:T(8,128)} %copy-done.1) | copy-start | bytes 2949124
  208.3 78.4 %all-to-all-start.3 = ((bf16[16,80,1280]{2,1,0:T(8,128)(2,1)}), bf16[16,80,1280]{2,1,0:T(8,128)(2,1)}, u32[]{:S(2)}, u32[]{:S(2)}) async-start(bf16[16,80,1280]{2,1,0:T(8,128)(2,1)} %bitcast.139), calls=%async_computation.3 | async-start | bytes 6553600 | tf_op jit(solution)/shard_map/all_to_all | solution.py:137
  215.1 2.5 copy-start.6
Sparse Core Ops, SparseCore 0:
  105.9 39.0 all-gather.2
  147.3 52.0 all-gather.4
